TPU v7x, 32 devices: a whole 2x2x4 slice. The times are simulated.
32 devices in a mesh: obs: 8 (over z, x), bel: 4 (over y, core).
Axes of the slice: x: 2, y: 2, z: 4, core: 2. Of those that a mesh axis runs over, the one named last changes fastest.
Arguments:
- alpha_set: bfloat16 [2048, 2048], P('bel'), may hold values from -600 to 600
- transitions: bfloat16 [16, 2048, 2048], P(None, 'obs'), may hold values from 0.0009994507 to 1
- obs_weights: float32 [256, 16, 2048], P('obs'), may hold values from 0.01 to 1
- rewards: float32 [16, 2048], replicated, may hold values from -1 to 1
- chosen_idx: int32 [1536, 16, 256], P('bel', None, 'obs'), may hold values from 0 to 2047
- chosen_action: int32 [1536], P('bel'), may hold values from 0 to 15
Outputs:
- new_alpha: float32 [1536, 2048], P(('bel', 'obs'))
Inputs may be any that keep to these rules, and one draw needn't show every extreme that they name: `chosen_idx`: an index into the 2048 alpha vectors. `chosen_action`: an index into the 16 actions.
All inputs are finite; a program needn't handle non-finite values.
Results may differ from a plain program's by a relative error of at most 0.0003.
Values may be sent and summed in bfloat16 or wider, within the bound.
A program may use at most 192 MiB of HBM per device.

v0:
```python
import jax
import jax.numpy as jnp
from jax import lax
from jax.sharding import PartitionSpec as P

discount = 0.95


def action_table(actions, count):
    return (actions[:, None] == jnp.arange(count, dtype=jnp.int32)[None, :]).astype(jnp.float32)


def picked_rows(indices, hot):
    chosen = jnp.sum(jnp.where(hot[:, :, None] > 0, indices, 0), axis=1)
    return chosen.T


def body(alpha_set, transitions, obs_weights, rewards, chosen_idx, chosen_action):
    actions = rewards.shape[0]
    states = rewards.shape[1]
    obs_local = obs_weights.shape[0]
    bel_rows = chosen_action.shape[0]
    trans_raw = transitions.astype(jnp.float32)
    action_hot = action_table(chosen_action, actions)
    picks = picked_rows(chosen_idx, action_hot).reshape(-1)
    piece = lax.all_gather(alpha_set, "bel", axis=0, tiled=True)
    count = piece.shape[0]
    onehot = (picks[:, None] == jnp.arange(count, dtype=jnp.int32)[None, :]).astype(jnp.bfloat16)
    chosen = jnp.dot(onehot, piece, preferred_element_type=jnp.float32)
    chosen = chosen.reshape(obs_local, bel_rows, states)
    obs_totals, trans_totals = lax.psum(
        (jnp.sum(obs_weights, axis=0), jnp.sum(trans_raw, axis=1)), "obs"
    )
    obs_prob = obs_weights / obs_totals[None, :, :]
    belief_prob = jnp.einsum("ba,oas->obs", action_hot, obs_prob, precision=lax.Precision.HIGHEST)
    partial_value = jnp.sum(belief_prob * chosen, axis=0)
    slice_w = lax.psum_scatter(partial_value, "obs", scatter_dimension=1, tiled=True)
    trans_prob = trans_raw / trans_totals[:, None, :]
    width = slice_w.shape[1]
    spread = (action_hot[:, :, None] * slice_w[:, None, :]).reshape(bel_rows, actions * width)
    table = trans_prob.reshape(actions * width, states)
    owned = bel_rows // lax.axis_size("obs")
    future = lax.psum_scatter(
        jnp.dot(spread, table, precision=lax.Precision.HIGHEST, preferred_element_type=jnp.float32),
        "obs",
        scatter_dimension=0,
        tiled=True,
    )
    own_hot = lax.dynamic_slice_in_dim(action_hot, lax.axis_index("obs") * owned, owned, 0)
    reward_rows = jnp.dot(
        own_hot, rewards, precision=lax.Precision.HIGHEST, preferred_element_type=jnp.float32
    )
    return reward_rows + discount * future


def solution(mesh):
    placed = (
        P("bel", None),
        P(None, "obs", None),
        P("obs", None, None),
        P(),
        P("bel", None, "obs"),
        P("bel"),
    )
    return jax.shard_map(
        body, mesh=mesh, in_specs=placed, out_specs=P(("bel", "obs"), None), check_vma=False
    )
```

profile of v0, /device:TPU:0, one launch (start us, length us, event | category | flops | bytes accessed | tf_op | source)
XLA Modules:
  0.0 457.6 jit_solution(5669605454711230280)
XLA Ops:
  7.4 0.0 copy-start
  7.4 0.0 all-gather.2.cloned.1.call-start
  7.4 0.7 all-gather.2.cloned.1.call-update
  8.1 0.0 all-reduce.3.cloned.1.call-start
  8.1 3.0 reduce_sum.36
  11.2 0.0 copy-start.3
  11.2 0.0 copy-start.1
  11.2 7.7 %convert_reduce_fusion = f32[16,2048]{1,0:T(8,128)} fusion(bf16[16,256,2048]{2,1,0:T(8,128)(2,1)} %param.7), kind=kLoop, calls=%fused_computation.6 | loop fusion | flops 16744448 | bytes 16908288 | tf_op jit(solution)/shard_map/reduce_sum | solution.py:32
  18.9 0.0 all-reduce.3.cloned.1.call-update
  18.9 0.0 reduce-scatter.3.cloned.1.call-start
  19.0 0.0 copy-done.3
  19.0 0.6 iota_compare_fusion.2
  19.6 0.0 copy-done.1
  19.6 0.1 select_reduce_fusion
  19.7 51.1 %all-gather.2.cloned.1.call-done = bf16[2048,2048]{1,0:T(8,128)(2,1)} async-done(((bf16[512,2048]{1,0:T(8,128)(2,1)}), bf16[2048,2048]{1,0:T(8,128)(2,1)}) %all-gather.2.cloned.1.call-update) | async-done | bytes 8388624 | tf_op jit(solution)/shard_map/all_gather | solution.py:26
  70.7 0.0 copy-start.4
  70.8 116.2 %fusion.1 = f32[12288,2048]{1,0:T(8,128)} fusion(bf16[2048,2048]{1,0:T(8,128)(2,1)} %all-gather.2.cloned.1.call-done, s32[12288]{0:T(1024)S(1)} %eq.38), kind=kOutput, calls=%fused_computation.3 | convolution fusion | flops 103104380928 | bytes 109101056 | tf_op jit(solution)/shard_map/dot_general | solution.py:29
  187.0 0.0 all-reduce.3.cloned.1.call-done
  187.0 0.0 copy-done.4
  187.0 0.0 copy-start.2
  187.0 62.6 %fusion = f32[384,2048]{1,0:T(8,128)} fusion(f32[32,384,2048]{2,1,0:T(8,128)} %bitcast.3, f32[32,16,2048]{2,1,0:T(8,128)} %param.8, f32[16,2048]{1,0:T(8,128)} %get-tuple-element.6, s32[384]{0:T(512)S(1)} %copy-done.4), kind=kOutput, calls=%fused_computation.1 | convolution fusion | flops 4882438144 | bytes 108135936 | tf_op jit(solution)/shard_map/ba,oas->obs/dot_general | solution.py:35
  249.6 0.0 copy-start.5
  249.6 0.0 reduce-scatter.3.cloned.1.call-update
  249.6 0.0 reduce-scatter.5.cloned.1.call-start
  249.6 75.1 %reduce-scatter.3.cloned.1.call-done = f32[384,256]{1,0:T(8,128)} async-done(((f32[384,2048]{1,0:T(8,128)}), f32[384,256]{1,0:T(8,128)}) %reduce-scatter.3.cloned.1.call-update) | async-done | bytes 393232 | tf_op jit(solution)/shard_map/reduce_scatter | solution.py:37
  324.8 0.0 copy-done.2
  324.8 1.9 fusion.30
  326.6 0.0 copy-done.5
  326.6 47.3 %fusion.9 = f32[384,2048]{1,0:T(8,128)} fusion(bf16[16,256,2048]{2,1,0:T(8,128)(2,1)} %param.7, f32[16,2048]{1,0:T(8,128)S(1)} %copy-done.5, f32[384,16,256]{2,0,1:T(8,128)S(1)} %fusion.30), kind=kOutput, calls=%fused_computation.13 | convolution fusion | flops 38671482880 | bytes 26345472 | tf_op jit(solution)/shard_map/dot_general | solution.py:44
  373.9 0.0 reduce-scatter.5.cloned.1.call-update
  374.0 73.8 %reduce-scatter.5.cloned.1.call-done = f32[48,2048]{1,0:T(8,128)} async-done(((f32[384,2048]{1,0:T(8,128)}), f32[48,2048]{1,0:T(8,128)}) %reduce-scatter.5.cloned.1.call-update) | async-done | bytes 393232 | tf_op jit(solution)/shard_map/reduce_scatter | solution.py:43
  447.8 0.0 copy-done
  447.8 2.2 convolution_add_fusion
  (1 shorter events, 0.0 us)
Async XLA Ops:
  7.4 440.4 %copy-start = (f32[16,2048]{1,0:T(8,128)S(1)}, f32[16,2048]{1,0:T(8,128)}, u32[]{:S(2)}) copy-start(f32[16,2048]{1,0:T(8,128)} %param.9) | copy-start | bytes 393220
  7.4 63.4 %all-gather.2.cloned.1.call-start = ((), (), s32[]{:S(2)}) async-start(), calls=%async_computation.2 | async-start | bytes 10485760 | tf_op jit(solution)/shard_map/all_gather | solution.py:26
  8.1 178.9 %all-reduce.3.cloned.1.call-start = ((), (), s32[]{:S(2)}) async-start(), calls=%async_computation.5 | async-start | bytes 524288 | tf_op jit(solution)/shard_map/psum | solution.py:31
  11.2 7.8 %copy-start.3 = (s32[384]{0:T(512)S(1)}, s32[384]{0:T(512)}, u32[]{:S(2)}) copy-start(s32[384]{0:T(512)} %param.11) | copy-start | bytes 4612
  11.2 8.4 %copy-start.1 = (s32[384,16,32]{0,2,1:T(8,128)S(1)}, s32[384,16,32]{0,2,1:T(8,128)}, u32[]{:S(2)}) copy-start(s32[384,16,32]{0,2,1:T(8,128)} %param.10) | copy-start | bytes 2359300
  18.9 305.8 %reduce-scatter.3.cloned.1.call-start = ((), (), s32[]{:S(2)}) async-start(), calls=%async_computation.3 | async-start | bytes 3538944 | tf_op jit(solution)/shard_map/reduce_scatter | solution.py:37
  70.7 116.2 %copy-start.4 = (s32[384]{0:T(512)S(1)}, s32[384]{0:T(512)}, u32[]{:S(2)}) copy-start(s32[384]{0:T(512)} %param.11) | copy-start | bytes 4612
  187.0 137.8 %copy-start.2 = (f32[384,16]{0,1:T(8,128)S(1)}, f32[384,16]{0,1:T(8,128)}, u32[]{:S(2)}) copy-start(f32[384,16]{0,1:T(8,128)} %get-tuple-element.9) | copy-start | bytes 73732
  249.6 77.1 %copy-start.5 = (f32[16,2048]{1,0:T(8,128)S(1)}, f32[16,2048]{1,0:T(8,128)}, u32[]{:S(2)}) copy-start(f32[16,2048]{1,0:T(8,128)} %get-tuple-element.5) | copy-start | bytes 393220
  249.6 198.2 %reduce-scatter.5.cloned.1.call-start = ((), (), s32[]{:S(2)}) async-start(), calls=%async_computation.4 | async-start | bytes 3538944 | tf_op jit(solution)/shard_map/reduce_scatter | solution.py:43
Sparse Core Ops, SparseCore 0:
  9.7 60.9 all-gather.1
Sparse Core Ops, SparseCore 1:
  19.0 74.0 all-reduce.2
  249.7 75.0 reduce-scatter.2
  374.1 73.7 reduce-scatter.4
where the time goes:
time: 458 us
  matrix products  228 us (50%)
  waiting for transfers between devices  201 us (44%)
  between operations  15.1 us (3%)
  other arithmetic  13.3 us (3%)
    dot_general x1, matrix products, body(): chosen = jnp.dot(onehot, piece, preferred_element_type=jnp.float32)  116 us
    reduce_scatter x1, waiting for transfers between devices, body(): lax.psum_scatter(partial_value, 'obs', scatter_dimension=1, tiled=True)  75.1 us
    reduce_scatter x1, waiting for transfers between devices, body(): lax.psum_scatter(jnp.dot(spread, table, precision=lax.Precision.HIGHEST,...  73.8 us
    dot_general x1, matrix products, body(): jnp.einsum('ba,oas->obs', action_hot, obs_prob, precision=lax.Precision.H...  62.6 us
    all_gather x1, waiting for transfers between devices, body(): piece = lax.all_gather(alpha_set, 'bel', axis=0, tiled=True)  51.1 us
    dot_general x1, matrix products, body(): jnp.dot(spread, table, precision=lax.Precision.HIGHEST, preferred_element...  47.3 us
  transfers between devices with their start and end apart: 4, of which 3 were waited for; matrix products, arithmetic and copies ran while one was open for 28% of the time, Pallas kernels for 0%

commit v1 on v0

v1 whole, which is shorter than its diff:
```python
import functools

import jax
import jax.numpy as jnp
from jax import lax
from jax.experimental import pallas as pl
from jax.experimental.pallas import tpu as pltpu
from jax.sharding import PartitionSpec as P

discount = 0.95
lanes = 128


def gather_kernel(picks_ref, act_ref, alpha_ref, weights_ref, out_ref):
    beliefs = act_ref.shape[0]
    obs_local = picks_ref.shape[0] // beliefs
    actions = weights_ref.shape[0] // obs_local
    slabs = alpha_ref.shape[1]
    rows = out_ref.shape[0] // slabs

    def one(b, carry):
        action = act_ref[b]
        sums = [None] * min(4, obs_local)
        for o in range(obs_local):
            row = alpha_ref[picks_ref[b * obs_local + o]].astype(jnp.float32)
            term = row * weights_ref[o * actions + action]
            at = o % len(sums)
            sums[at] = term if sums[at] is None else sums[at] + term
        out_ref[pl.ds(b, slabs, stride=rows), :] = functools.reduce(jnp.add, sums)
        return carry

    lax.fori_loop(0, beliefs, one, 0)

    def total(a, carry):
        acc = weights_ref[a]
        for o in range(1, obs_local):
            acc = acc + weights_ref[o * actions + a]
        out_ref[pl.ds(beliefs + a, slabs, stride=rows), :] = acc
        return carry

    lax.fori_loop(0, actions, total, 0)


def gather_rows(picks, acts, alpha, weights):
    slabs = alpha.shape[1]
    beliefs = acts.shape[0]
    actions = 1 if beliefs == 0 else weights.shape[0] // (picks.shape[0] // beliefs)
    rows = beliefs + actions
    vmem = pl.BlockSpec(memory_space=pltpu.VMEM)
    smem = pl.BlockSpec(memory_space=pltpu.SMEM)
    out = pl.pallas_call(
        gather_kernel,
        out_shape=jax.ShapeDtypeStruct((slabs * rows, lanes), jnp.float32),
        in_specs=[smem, smem, vmem, vmem],
        out_specs=vmem,
        compiler_params=pltpu.CompilerParams(vmem_limit_bytes=40 << 20),
        cost_estimate=pl.CostEstimate(
            flops=80_000_000, bytes_accessed=16 << 20, transcendentals=0
        ),
        name="gather_rows",
    )(picks, acts, alpha, weights)
    return out.reshape(slabs, rows, lanes)


def move_kernel(act_ref, w_ref, tot_ref, table_ref, out_ref):
    a = pl.program_id(0)
    scaled = w_ref[...] / tot_ref[0]
    x = jnp.where(act_ref[...] == a, scaled, 0.0)
    high = x.astype(jnp.bfloat16)
    low = (x - high.astype(jnp.float32)).astype(jnp.bfloat16)
    table = table_ref[0]
    both = jnp.dot(jnp.concatenate([high, low], axis=0), table, preferred_element_type=jnp.float32)
    half = x.shape[0]
    part = both[:half] + both[half:]

    @pl.when(a == 0)
    def _():
        out_ref[...] = part

    @pl.when(a > 0)
    def _():
        out_ref[...] += part


def move(acts, weighted, totals, table):
    beliefs, width = weighted.shape
    actions, _, states = table.shape
    return pl.pallas_call(
        move_kernel,
        grid=(actions,),
        out_shape=jax.ShapeDtypeStruct((beliefs, states), jnp.float32),
        in_specs=[
            pl.BlockSpec((beliefs, 1), lambda a: (0, 0)),
            pl.BlockSpec((beliefs, width), lambda a: (0, 0)),
            pl.BlockSpec((1, 1, width), lambda a: (a, 0, 0)),
            pl.BlockSpec((1, width, states), lambda a: (a, 0, 0)),
        ],
        out_specs=pl.BlockSpec((beliefs, states), lambda a: (0, 0)),
        compiler_params=pltpu.CompilerParams(
            vmem_limit_bytes=48 << 20, dimension_semantics=("arbitrary",)
        ),
        cost_estimate=pl.CostEstimate(
            flops=4 * beliefs * width * actions * states,
            bytes_accessed=2 * actions * width * states,
            transcendentals=0,
        ),
        name="move",
    )(acts[:, None], weighted, totals[:, None, :], table)


def action_table(actions, count):
    return (actions[:, None] == jnp.arange(count, dtype=jnp.int32)[None, :]).astype(jnp.float32)


def body(alpha_set, transitions, obs_weights, rewards, chosen_idx, chosen_action):
    actions, states = rewards.shape
    obs_local = obs_weights.shape[0]
    beliefs = chosen_action.shape[0]
    slabs = states // lanes
    ranks = lax.axis_size("obs")
    action_hot = action_table(chosen_action, actions)
    picks = jnp.sum(jnp.where(action_hot[:, :, None] > 0, chosen_idx, 0), axis=1).reshape(-1)
    alpha = lax.all_gather(alpha_set.reshape(-1, slabs, lanes), "bel", axis=0, tiled=True)
    weights = obs_weights.reshape(obs_local * actions, slabs, lanes)
    trans_totals = lax.psum(jnp.sum(transitions.astype(jnp.float32), axis=1), "obs")
    partial = gather_rows(picks, chosen_action, alpha, weights)
    if slabs % ranks == 0:
        piece = lax.psum_scatter(partial, "obs", scatter_dimension=0, tiled=True)
        piece = piece.transpose(1, 0, 2).reshape(beliefs + actions, -1)
    else:
        flat = partial.transpose(1, 0, 2).reshape(beliefs + actions, states)
        piece = lax.psum_scatter(flat, "obs", scatter_dimension=1, tiled=True)
    moved = move(chosen_action, piece[:beliefs], piece[beliefs:], transitions)
    future = lax.psum_scatter(moved, "obs", scatter_dimension=0, tiled=True)
    owned = beliefs // ranks
    own_hot = lax.dynamic_slice_in_dim(action_hot, lax.axis_index("obs") * owned, owned, 0)
    own = functools.partial(
        jnp.dot, own_hot, precision=lax.Precision.HIGHEST, preferred_element_type=jnp.float32
    )
    return own(rewards) + discount * (future / own(trans_totals))


def solution(mesh):
    placed = (
        P("bel", None),
        P(None, "obs", None),
        P("obs", None, None),
        P(),
        P("bel", None, "obs"),
        P("bel"),
    )
    return jax.shard_map(
        body, mesh=mesh, in_specs=placed, out_specs=P(("bel", "obs"), None), check_vma=False
    )
```

time: 458 us -> 332 us (0.72)
  matrix products: 228 us -> 2.69 us
  Pallas kernels: 0 us -> 47.1 us
  waiting for transfers between devices: 201 us -> 247 us
  local copies, waits for them, and re-layouts: 0.03 us -> 13 us
  other arithmetic: 13.3 us -> 7.73 us
    dot_general x4 -> x2, matrix products: 228 us -> 2.69 us  [body(): return own(rewards) + discount * (future / own(trans_totals))]
    pallas_call x0 -> x2, Pallas kernels: none -> 47.1 us  [the longest x1 24.6 us: move(): pl.pallas_call(move_kernel, grid=(actions,), out_shape=jax.ShapeDtypeStru...]
    psum x1, waiting for transfers between devices: 0.01 us -> 46.4 us  [body(): lax.psum(jnp.sum(transitions.astype(jnp.float32), axis=1), 'obs')]
    unnamed x12 -> x10, local copies, waits for them, and re-layouts: 0.02 us -> 10.9 us
    all_gather x1, waiting for transfers between devices: 51.1 us -> 55.7 us  [body(): lax.all_gather(alpha_set.reshape(-1, slabs, lanes), 'bel', axis=0, tiled=...]
    reduce_sum x3 -> x2, other arithmetic: 10.8 us -> 7.72 us  [the longest x1 7.64 us: body(): jnp.sum(transitions.astype(jnp.float32), axis=1)]
  transfers between devices with their start and end apart: 4 -> 4, of which waited for: 3 -> 4; matrix products, arithmetic and copies ran while one was open for 28% -> 4% of each run, Pallas kernels for 0% -> 7%
where the time goes in v1:
time: 332 us; the launch traced here: 331 us
  waiting for transfers between devices  247 us (74%)
  Pallas kernels  47.1 us (14%)
  between operations  13.2 us (4%)
  local copies, waits for them, and re-layouts  13 us (4%)
  other arithmetic  7.73 us (2%)
    reduce_scatter x1, waiting for transfers between devices, body(): future = lax.psum_scatter(moved, 'obs', scatter_dimension=0, tiled=True)  76.9 us
    reduce_scatter x1, waiting for transfers between devices, body(): piece = lax.psum_scatter(partial, 'obs', scatter_dimension=0, tiled=True)  68.3 us
    all_gather x1, waiting for transfers between devices, body(): lax.all_gather(alpha_set.reshape(-1, slabs, lanes), 'bel', axis=0, tiled=...  55.7 us
    psum x1, waiting for transfers between devices, body(): lax.psum(jnp.sum(transitions.astype(jnp.float32), axis=1), 'obs')  46.4 us
    pallas_call x1, Pallas kernels, move(): pl.pallas_call(move_kernel, grid=(actions,), out_shape=jax.ShapeDtypeStru...  24.6 us
    pallas_call x1, Pallas kernels, gather_rows(): pl.pallas_call(gather_kernel, out_shape=jax.ShapeDtypeStruct((slabs * row...  22.5 us
    unnamed x10, local copies, waits for them, and re-layouts  10.9 us
    reduce_sum x1, other arithmetic, body(): jnp.sum(transitions.astype(jnp.float32), axis=1)  7.64 us
  transfers between devices with their start and end apart: 4, of which 4 were waited for; matrix products, arithmetic and copies ran while one was open for 4% of the time, Pallas kernels for 7%

profile of v1, /device:TPU:0, one launch (start us, length us, event | category | flops | bytes accessed | tf_op | source)
XLA Modules:
  0.0 331.3 jit_solution(17208599002347701231)
XLA Ops:
  6.5 0.0 copy-start
  6.5 0.0 copy-start.2
  6.5 0.0 copy-start.3
  6.5 0.0 all-gather.2.cloned.1.call-start
  6.5 3.6 %copy.15 = bf16[64,8,16,128]{3,2,1,0:T(8,128)(2,1)} copy(bf16[64,8,16,128]{3,1,2,0:T(8,128)(2,1)} %bitcast.19) | data formatting | bytes 4194304
  10.2 0.0 all-gather.2.cloned.1.call-update
  10.2 0.0 reduce-scatter.3.cloned.1.call-start
  10.3 0.0 copy-done.2
  10.3 0.0 copy-done.3
  10.3 0.1 select_reduce_fusion
  10.4 0.1 copy.10
  10.5 0.1 reshape.39.picks_ref
  10.6 5.1 %copy.16 = f32[64,8,16,128]{3,2,1,0:T(8,128)} copy(f32[64,8,16,128]{3,1,2,0:T(8,128)} %bitcast.18) | data formatting | bytes 8388608
  15.7 55.7 %all-gather.2.cloned.1.call-done.alpha_ref = bf16[2048,16,128]{2,1,0:T(8,128)(2,1)} async-done(((bf16[512,16,128]{2,1,0:T(8,128)(2,1)}), bf16[2048,16,128]{2,1,0:T(8,128)(2,1)}) %all-gather.2.cloned.1.call-update) | async-done | bytes 8388624 | tf_op jit(solution)/shard_map/all_gather | solution.py:123
  71.4 0.0 copy-start.1
  71.4 2.2 copy-done.1
  73.5 22.5 %gather_rows.1 = f32[6400,128]{1,0:T(8,128)} custom-call(s32[12288]{0:T(1024)S(1)} %reshape.39.picks_ref, s32[384]{0:T(512)S(1)} %copy-done.2, bf16[2048,16,128]{2,1,0:T(8,128)(2,1)} %all-gather.2.cloned.1.call-done.alpha_ref, f32[512,16,128]{2,1,0:T(8,128)S(1)} %bitcast.15), custom_call_target="tpu_custom_call" | custom-call | flops 80000000 | bytes 16777216 | tf_op jit(solution)/shard_map/gather_rows/pallas_call | solution.py:51
  96.1 0.0 reduce-scatter.3.cloned.1.call-update
  96.1 0.0 all-reduce.2.cloned.1.call-start
  96.1 7.6 %convert_reduce_fusion = f32[16,2048]{1,0:T(8,128)} fusion(bf16[16,256,2048]{2,1,0:T(8,128)(2,1)} %table_ref.1), kind=kLoop, calls=%fused_computation | loop fusion | flops 16744448 | bytes 16908288 | tf_op jit(solution)/shard_map/reduce_sum | solution.py:125
  103.8 0.0 all-reduce.2.cloned.1.call-update
  103.8 0.0 reduce-scatter.5.cloned.1.call-start
  103.8 0.1 broadcast_in_dim.25.act_ref
  104.0 68.3 %reduce-scatter.3.cloned.1.call-done = f32[2,400,128]{2,1,0:T(8,128)} async-done(((f32[16,400,128]{2,1,0:T(8,128)}), f32[2,400,128]{2,1,0:T(8,128)}) %reduce-scatter.3.cloned.1.call-update) | async-done | bytes 409616 | tf_op jit(solution)/shard_map/reduce_scatter | solution.py:128
  172.3 1.0 copy_bitcast_fusion.w_ref
  173.3 0.7 slice.14
  174.1 24.6 %move.1 = f32[384,2048]{1,0:T(8,128)} custom-call(s32[384,1]{1,0:T(8,128)S(1)} %broadcast_in_dim.25.act_ref, f32[384,256]{1,0:T(8,128)S(1)} %copy_bitcast_fusion.w_ref, f32[16,1,256]{2,1,0:T(1,128)S(1)} %bitcast.16, bf16[16,256,2048]{2,1,0:T(8,128)(2,1)} %table_ref.1), custom_call_target="tpu_custom_call" | custom-call | flops 12884901888 | bytes 16777216 | tf_op jit(solution)/shard_map/move/pallas_call | solution.py:88
  198.7 0.0 reduce-scatter.5.cloned.1.call-update
  198.7 46.4 %all-reduce.2.cloned.1.call-done = f32[16,2048]{1,0:T(8,128)} async-done(((f32[16,2048]{1,0:T(8,128)}), f32[16,2048]{1,0:T(8,128)}) %all-reduce.2.cloned.1.call-update) | async-done | bytes 131088 | tf_op jit(solution)/shard_map/psum | solution.py:125
  245.1 76.9 %reduce-scatter.5.cloned.1.call-done = f32[48,2048]{1,0:T(8,128)} async-done(((f32[384,2048]{1,0:T(8,128)}), f32[48,2048]{1,0:T(8,128)}) %reduce-scatter.5.cloned.1.call-update) | async-done | bytes 393232 | tf_op jit(solution)/shard_map/reduce_scatter | solution.py:134
  322.1 1.5 fusion
  323.6 0.0 copy-done
  323.6 1.2 convolution_add_fusion
  (2 shorter events, 0.0 us)
Async XLA Ops:
  6.5 317.0 %copy-start = (f32[16,2048]{1,0:T(8,128)S(1)}, f32[16,2048]{1,0:T(8,128)}, u32[]{:S(2)}) copy-start(f32[16,2048]{1,0:T(8,128)} %param.9) | copy-start | bytes 393220
  6.5 3.7 %copy-start.2 = (s32[384]{0:T(512)S(1)}, s32[384]{0:T(512)}, u32[]{:S(2)}) copy-start(s32[384]{0:T(512)} %act_ref.1) | copy-start | bytes 4612
  6.5 3.8 %copy-start.3 = (s32[384,16,32]{0,2,1:T(8,128)S(1)}, s32[384,16,32]{0,2,1:T(8,128)}, u32[]{:S(2)}) copy-start(s32[384,16,32]{0,2,1:T(8,128)} %param.10) | copy-start | bytes 2359300
  6.5 64.8 %all-gather.2.cloned.1.call-start = ((), (), s32[]{:S(2)}) async-start(), calls=%async_computation.2 | async-start | bytes 10485760 | tf_op jit(solution)/shard_map/all_gather | solution.py:123
  10.2 162.1 %reduce-scatter.3.cloned.1.call-start = ((), (), s32[]{:S(2)}) async-start(), calls=%async_computation.3 | async-start | bytes 3686400 | tf_op jit(solution)/shard_map/reduce_scatter | solution.py:128
  71.4 2.2 copy-start.1
  96.1 149.0 %all-reduce.2.cloned.1.call-start = ((), (), s32[]{:S(2)}) async-start(), calls=%async_computation.5 | async-start | bytes 262144 | tf_op jit(solution)/shard_map/psum | solution.py:125
  103.8 218.3 %reduce-scatter.5.cloned.1.call-start = ((), (), s32[]{:S(2)}) async-start(), calls=%async_computation.4 | async-start | bytes 3538944 | tf_op jit(solution)/shard_map/reduce_scatter | solution.py:134
Sparse Core Ops, SparseCore 0:
  10.3 60.9 all-gather.1
  96.2 76.0 reduce-scatter.2
  175.7 69.4 all-reduce.1
  248.6 73.4 reduce-scatter.4

commit v2 on v1

--- a/solution.py
+++ b/solution.py
@@ -11,7 +11,7 @@
 lanes = 128
 
 
-def gather_kernel(picks_ref, act_ref, alpha_ref, weights_ref, out_ref):
+def gather_kernel(picks_ref, act_ref, alpha_ref, weights_ref, moves_ref, out_ref):
     beliefs = act_ref.shape[0]
     obs_local = picks_ref.shape[0] // beliefs
     actions = weights_ref.shape[0] // obs_local
@@ -36,29 +36,29 @@
         for o in range(1, obs_local):
             acc = acc + weights_ref[o * actions + a]
         out_ref[pl.ds(beliefs + a, slabs, stride=rows), :] = acc
+        out_ref[pl.ds(beliefs + actions + a, slabs, stride=rows), :] = moves_ref[a]
         return carry
 
     lax.fori_loop(0, actions, total, 0)
 
 
-def gather_rows(picks, acts, alpha, weights):
+def gather_rows(picks, acts, alpha, weights, moves):
     slabs = alpha.shape[1]
     beliefs = acts.shape[0]
-    actions = 1 if beliefs == 0 else weights.shape[0] // (picks.shape[0] // beliefs)
-    rows = beliefs + actions
+    rows = beliefs + 2 * moves.shape[0]
     vmem = pl.BlockSpec(memory_space=pltpu.VMEM)
     smem = pl.BlockSpec(memory_space=pltpu.SMEM)
     out = pl.pallas_call(
         gather_kernel,
         out_shape=jax.ShapeDtypeStruct((slabs * rows, lanes), jnp.float32),
-        in_specs=[smem, smem, vmem, vmem],
+        in_specs=[smem, smem, vmem, vmem, vmem],
         out_specs=vmem,
         compiler_params=pltpu.CompilerParams(vmem_limit_bytes=40 << 20),
         cost_estimate=pl.CostEstimate(
             flops=80_000_000, bytes_accessed=16 << 20, transcendentals=0
         ),
         name="gather_rows",
-    )(picks, acts, alpha, weights)
+    )(picks, acts, alpha, weights, moves)
     return out.reshape(slabs, rows, lanes)
 
 
@@ -122,15 +122,19 @@
     picks = jnp.sum(jnp.where(action_hot[:, :, None] > 0, chosen_idx, 0), axis=1).reshape(-1)
     alpha = lax.all_gather(alpha_set.reshape(-1, slabs, lanes), "bel", axis=0, tiled=True)
     weights = obs_weights.reshape(obs_local * actions, slabs, lanes)
-    trans_totals = lax.psum(jnp.sum(transitions.astype(jnp.float32), axis=1), "obs")
-    partial = gather_rows(picks, chosen_action, alpha, weights)
+    trans_part = jnp.sum(transitions.astype(jnp.float32), axis=1).reshape(actions, slabs, lanes)
+    partial = gather_rows(picks, chosen_action, alpha, weights, trans_part)
+    rows = partial.shape[1]
     if slabs % ranks == 0:
         piece = lax.psum_scatter(partial, "obs", scatter_dimension=0, tiled=True)
-        piece = piece.transpose(1, 0, 2).reshape(beliefs + actions, -1)
+        piece = piece.transpose(1, 0, 2).reshape(rows, -1)
     else:
-        flat = partial.transpose(1, 0, 2).reshape(beliefs + actions, states)
+        flat = partial.transpose(1, 0, 2).reshape(rows, states)
         piece = lax.psum_scatter(flat, "obs", scatter_dimension=1, tiled=True)
-    moved = move(chosen_action, piece[:beliefs], piece[beliefs:], transitions)
+    trans_totals = lax.all_gather(piece[beliefs + actions :], "obs", axis=1, tiled=True)
+    moved = move(
+        chosen_action, piece[:beliefs], piece[beliefs : beliefs + actions], transitions
+    )
     future = lax.psum_scatter(moved, "obs", scatter_dimension=0, tiled=True)
     owned = beliefs // ranks
     own_hot = lax.dynamic_slice_in_dim(action_hot, lax.axis_index("obs") * owned, owned, 0)

time: 332 us -> 286 us (0.86)
  waiting for transfers between devices: 247 us -> 169 us
  blocking collectives: 0 us -> 31.3 us
    psum x1 -> x0, waiting for transfers between devices: 46.4 us -> none  [body(): lax.psum(jnp.sum(transitions.astype(jnp.float32), axis=1), 'obs')]
    reduce_scatter x1, waiting for transfers between devices: 76.9 us -> 43.4 us  [body(): future = lax.psum_scatter(moved, 'obs', scatter_dimension=0, tiled=True)]
    all_gather x0 -> x1, blocking collectives: none -> 31.3 us  [body(): lax.all_gather(piece[beliefs + actions:], 'obs', axis=1, tiled=True)]
    reduce_scatter x1, waiting for transfers between devices: 68.3 us -> 77.9 us  [body(): piece = lax.psum_scatter(partial, 'obs', scatter_dimension=0, tiled=True)]
    all_gather x1, waiting for transfers between devices: 55.7 us -> 47.7 us  [body(): lax.all_gather(alpha_set.reshape(-1, slabs, lanes), 'bel', axis=0, tiled=...]
    unnamed x10 -> x12, local copies, waits for them, and re-layouts: 10.9 us -> 11.7 us
  transfers between devices with their start and end apart: 4 -> 3, of which waited for: 4 -> 3; matrix products, arithmetic and copies ran while one was open for 4% -> 5% of each run, Pallas kernels for 7% -> 0%
where the time goes in v2:
time: 286 us; the launch traced here: 285 us
  waiting for transfers between devices  169 us (59%)
  Pallas kernels  48.2 us (17%)
  blocking collectives  31.3 us (11%)
  between operations  13.2 us (5%)
  local copies, waits for them, and re-layouts  13 us (5%)
  other arithmetic  8.04 us (3%)
    reduce_scatter x1, waiting for transfers between devices, body(): piece = lax.psum_scatter(partial, 'obs', scatter_dimension=0, tiled=True)  77.9 us
    all_gather x1, waiting for transfers between devices, body(): lax.all_gather(alpha_set.reshape(-1, slabs, lanes), 'bel', axis=0, tiled=...  47.7 us
    reduce_scatter x1, waiting for transfers between devices, body(): future = lax.psum_scatter(moved, 'obs', scatter_dimension=0, tiled=True)  43.4 us
    all_gather x1, blocking collectives, body(): lax.all_gather(piece[beliefs + actions:], 'obs', axis=1, tiled=True)  31.3 us
    pallas_call x1, Pallas kernels, move(): pl.pallas_call(move_kernel, grid=(actions,), out_shape=jax.ShapeDtypeStru...  24.6 us
    pallas_call x1, Pallas kernels, gather_rows(): pl.pallas_call(gather_kernel, out_shape=jax.ShapeDtypeStruct((slabs * row...  23.5 us
    unnamed x12, local copies, waits for them, and re-layouts  11.7 us
    reduce_sum x1, other arithmetic, body(): jnp.sum(transitions.astype(jnp.float32), axis=1)  7.95 us
  transfers between devices with their start and end apart: 3, of which 3 were waited for; matrix products, arithmetic and copies ran while one was open for 5% of the time, Pallas kernels for 0%

profile of v2, /device:TPU:0, one launch (start us, length us, event | category | flops | bytes accessed | tf_op | source)
XLA Modules:
  0.0 285.4 jit_solution(14449361546637342965)
XLA Ops:
  6.5 0.0 copy-start
  6.5 0.0 copy-start.2
  6.5 0.0 copy-start.3
  6.5 0.0 all-gather.2.cloned.1.call-start
  6.5 3.6 %copy.21 = bf16[64,8,16,128]{3,2,1,0:T(8,128)(2,1)} copy(bf16[64,8,16,128]{3,1,2,0:T(8,128)(2,1)} %bitcast.27) | data formatting | bytes 4194304
  10.2 0.0 all-gather.2.cloned.1.call-update
  10.2 0.0 reduce-scatter.3.cloned.1.call-start
  10.3 0.0 copy-done.2
  10.3 0.0 copy-done.3
  10.3 0.1 select_reduce_fusion
  10.4 0.1 copy.14
  10.5 0.1 reshape.43.picks_ref
  10.6 5.1 %copy.22 = f32[64,8,16,128]{3,2,1,0:T(8,128)} copy(f32[64,8,16,128]{3,1,2,0:T(8,128)} %bitcast.26) | data formatting | bytes 8388608
  15.7 8.0 %convert_reduce_fusion = f32[16,2048]{1,0:T(8,128)S(1)} fusion(bf16[16,256,2048]{2,1,0:T(8,128)(2,1)} %table_ref.1), kind=kLoop, calls=%fused_computation | loop fusion | flops 16744448 | bytes 16908288 | tf_op jit(solution)/shard_map/reduce_sum | solution.py:125
  23.7 47.7 %all-gather.2.cloned.1.call-done.alpha_ref = bf16[2048,16,128]{2,1,0:T(8,128)(2,1)} async-done(((bf16[512,16,128]{2,1,0:T(8,128)(2,1)}), bf16[2048,16,128]{2,1,0:T(8,128)(2,1)}) %all-gather.2.cloned.1.call-update) | async-done | bytes 8388624 | tf_op jit(solution)/shard_map/all_gather | solution.py:123
  71.3 0.0 copy-start.1
  71.3 2.2 copy-done.1
  73.5 23.5 %gather_rows.1 = f32[6656,128]{1,0:T(8,128)} custom-call(s32[12288]{0:T(1024)S(1)} %reshape.43.picks_ref, s32[384]{0:T(512)S(1)} %copy-done.2, bf16[2048,16,128]{2,1,0:T(8,128)(2,1)} %all-gather.2.cloned.1.call-done.alpha_ref, f32[512,16,128]{2,1,0:T(8,128)S(1)} %bitcast.22, f32[16,16,128]{2,1,0:T(8,128)S(1)} %bitcast.23), custom_call_target="tpu_custom_call" | custom-call | flops 80000000 | bytes 16777216 | tf_op jit(solution)/shard_map/gather_rows/pallas_call | solution.py:51
  97.1 0.0 reduce-scatter.3.cloned.1.call-update
  97.1 0.0 reduce-scatter.5.cloned.1.call-start
  97.2 0.1 broadcast_in_dim.25.act_ref
  97.3 77.9 %reduce-scatter.3.cloned.1.call-done = f32[2,416,128]{2,1,0:T(8,128)} async-done(((f32[16,416,128]{2,1,0:T(8,128)}), f32[2,416,128]{2,1,0:T(8,128)}) %reduce-scatter.3.cloned.1.call-update) | async-done | bytes 426000 | tf_op jit(solution)/shard_map/reduce_scatter | solution.py:129
  175.2 0.7 slice_bitcast_fusion.1
  175.9 1.0 copy_bitcast_fusion.w_ref
  176.9 24.6 %move.1 = f32[384,2048]{1,0:T(8,128)} custom-call(s32[384,1]{1,0:T(8,128)S(1)} %broadcast_in_dim.25.act_ref, f32[384,256]{1,0:T(8,128)S(1)} %copy_bitcast_fusion.w_ref, f32[16,1,256]{2,1,0:T(1,128)S(1)} %bitcast.24, bf16[16,256,2048]{2,1,0:T(8,128)(2,1)} %table_ref.1), custom_call_target="tpu_custom_call" | custom-call | flops 12884901888 | bytes 16777216 | tf_op jit(solution)/shard_map/move/pallas_call | solution.py:88
  201.5 0.0 reduce-scatter.5.cloned.1.call-update
  201.6 31.3 %all_gather.7 = f32[16,2048]{1,0:T(8,128)S(1)} all-gather(f32[16,256]{1,0:T(8,128)S(1)} %bitcast.31), channel_id=1, replica_groups=mesh['obs'=8,'bel'=4] {'obs'}, dimensions={1}, use_global_device_ids=true | all-gather | bytes 147456 | tf_op jit(solution)/shard_map/all_gather | solution.py:134
  232.9 43.4 %reduce-scatter.5.cloned.1.call-done = f32[48,2048]{1,0:T(8,128)} async-done(((f32[384,2048]{1,0:T(8,128)}), f32[48,2048]{1,0:T(8,128)}) %reduce-scatter.5.cloned.1.call-update) | async-done | bytes 393232 | tf_op jit(solution)/shard_map/reduce_scatter | solution.py:138
  276.2 1.4 fusion
  277.7 0.0 copy-done
  277.7 1.2 convolution_add_fusion
  (4 shorter events, 0.1 us)
Async XLA Ops:
  6.5 271.1 %copy-start = (f32[16,2048]{1,0:T(8,128)S(1)}, f32[16,2048]{1,0:T(8,128)}, u32[]{:S(2)}) copy-start(f32[16,2048]{1,0:T(8,128)} %param.9) | copy-start | bytes 393220
  6.5 3.7 %copy-start.2 = (s32[384]{0:T(512)S(1)}, s32[384]{0:T(512)}, u32[]{:S(2)}) copy-start(s32[384]{0:T(512)} %act_ref.1) | copy-start | bytes 4612
  6.5 3.7 %copy-start.3 = (s32[384,16,32]{0,2,1:T(8,128)S(1)}, s32[384,16,32]{0,2,1:T(8,128)}, u32[]{:S(2)}) copy-start(s32[384,16,32]{0,2,1:T(8,128)} %param.10) | copy-start | bytes 2359300
  6.5 64.8 %all-gather.2.cloned.1.call-start = ((), (), s32[]{:S(2)}) async-start(), calls=%async_computation.2 | async-start | bytes 10485760 | tf_op jit(solution)/shard_map/all_gather | solution.py:123
  10.2 165.0 %reduce-scatter.3.cloned.1.call-start = ((), (), s32[]{:S(2)}) async-start(), calls=%async_computation.3 | async-start | bytes 3833856 | tf_op jit(solution)/shard_map/reduce_scatter | solution.py:129
  71.3 2.2 copy-start.1
  97.1 179.1 %reduce-scatter.5.cloned.1.call-start = ((), (), s32[]{:S(2)}) async-start(), calls=%async_computation.4 | async-start | bytes 3538944 | tf_op jit(solution)/shard_map/reduce_scatter | solution.py:138
Sparse Core Ops, SparseCore 0:
  10.3 60.9 all-gather.1
  97.2 77.8 reduce-scatter.2
  201.7 74.4 reduce-scatter.4
